TPU v7x, 32 devices: a whole 2x2x4 slice. The times are simulated.
32 devices in a mesh: dp: 8 (over y, x, core), seq: 4 (over z).
Axes of the slice: x: 2, y: 2, z: 4, core: 2. Of those that a mesh axis runs over, the one named last changes fastest.
Arguments:
- tokens: bfloat16 [16384, 1024], P(('dp', 'seq')), may hold values from -6 to 6
- cotangent: bfloat16 [16384, 1024], P(('dp', 'seq')), may hold values from -6 to 6
- qkv_weight: bfloat16 [1024, 3072], replicated, may hold values from -0.1875 to 0.1875
- proj_weight: bfloat16 [1024, 1024], replicated, may hold values from -0.75 to 0.75
- up_weight: bfloat16 [1024, 4096], replicated, may hold values from -0.1875 to 0.1875
- down_weight: bfloat16 [4096, 1024], replicated, may hold values from -0.09375 to 0.09375
- norm_gains: float32 [2, 1024], replicated, may hold values from 0.5 to 1.5
- biases: float32 [6, 1024], replicated, may hold values from -1.5 to 1.5
- up_bias: float32 [4096], replicated, may hold values from -1.5 to 1.5
- head_slopes: float32 [16], replicated, may hold values from 0.00012207031 to 0.5, as said below
- qkv_moment: float32 [1024, 3072], P(None, 'dp'), may hold values from -1536 to 1536
- proj_moment: float32 [1024, 1024], P(None, 'dp'), may hold values from -1536 to 1536
- up_moment: float32 [1024, 4096], P(None, 'dp'), may hold values from -1536 to 1536
- down_moment: float32 [4096, 1024], P('dp'), may hold values from -1536 to 1536
- gains_moment: float32 [2, 1024], P(None, 'dp'), may hold values from -768 to 768
- biases_moment: float32 [6, 1024], P(None, 'dp'), may hold values from -768 to 768
- upbias_moment: float32 [4096], P('dp'), may hold values from -768 to 768
Outputs:
- block_out: bfloat16 [16384, 1024], P(('dp', 'seq'))
- tokens_grad: float32 [16384, 1024], P(('dp', 'seq'))
- qkv_grad: float32 [1024, 3072], P(None, 'dp')
- proj_grad: float32 [1024, 1024], P(None, 'dp')
- up_grad: float32 [1024, 4096], P(None, 'dp')
- down_grad: float32 [4096, 1024], P('dp')
- gains_grad: float32 [2, 1024], P(None, 'dp')
- biases_grad: float32 [6, 1024], P(None, 'dp')
- upbias_grad: float32 [4096], P('dp')
- qkv_state: float32 [1024, 3072], P(None, 'dp')
- proj_state: float32 [1024, 1024], P(None, 'dp')
- up_state: float32 [1024, 4096], P(None, 'dp')
- down_state: float32 [4096, 1024], P('dp')
- gains_state: float32 [2, 1024], P(None, 'dp')
- biases_state: float32 [6, 1024], P(None, 'dp')
- upbias_state: float32 [4096], P('dp')
- qkv_new: float32 [1024, 3072], P(None, 'dp')
- proj_new: float32 [1024, 1024], P(None, 'dp')
- up_new: float32 [1024, 4096], P(None, 'dp')
- down_new: float32 [4096, 1024], P('dp')
- gains_new: float32 [2, 1024], P(None, 'dp')
- biases_new: float32 [6, 1024], P(None, 'dp')
- upbias_new: float32 [4096], P('dp')
Inputs may be any that keep to these rules, and one draw needn't show every extreme that they name: `head_slopes`: one positive slope a head.
All inputs are finite; a program needn't handle non-finite values.
Results may differ from a plain program's by a relative error of at most 0.025.
Values may be sent and summed in bfloat16 or wider, within the bound.
A program may use at most 256 MiB of HBM per device.

v0:
```python
import math
import jax
import jax.numpy as jnp
from jax import lax
from jax.sharding import PartitionSpec as P

NS_ITERS = 5
MOMENTUM = 0.9
RATE_MATRIX = 0.2
RATE_VECTOR = 0.0015
NORM_EPS = 1e-05
ORTHO_EPS = 1e-07
COEF_A = 2.0
COEF_B = -1.0
GELU_C = 0.7978845608028654
MASKED = -1e30


def norm_forward(values, gain_row, offset):
    center = values - jnp.mean(values, axis=-1, keepdims=True)
    inv_scale = lax.rsqrt(jnp.mean(center * center, axis=-1, keepdims=True) + NORM_EPS)
    unit_values = center * inv_scale
    return (unit_values * gain_row + offset, unit_values, inv_scale)


def norm_backward(upstream, unit_values, inv_scale, gain_row):
    scaled = upstream * gain_row
    inner_sum = jnp.mean(scaled * unit_values, axis=-1, keepdims=True)
    input_grad = inv_scale * (
        scaled - jnp.mean(scaled, axis=-1, keepdims=True) - unit_values * inner_sum
    )
    return (input_grad, jnp.sum(upstream * unit_values, axis=0), jnp.sum(upstream, axis=0))


def gelu_tanh(values):
    return 0.5 * values * (1.0 + jnp.tanh(GELU_C * (values + 0.044715 * values * values * values)))


def gelu_slope(values):
    tangent = jnp.tanh(GELU_C * (values + 0.044715 * values * values * values))
    return 0.5 * (1.0 + tangent) + 0.5 * values * (1.0 - tangent * tangent) * GELU_C * (
        1.0 + 3.0 * 0.044715 * values * values
    )


def contract_rows(left, right):
    return lax.dot_general(
        left, right, (((0,), (0,)), ((), ())), preferred_element_type=jnp.float32
    )


def contract_cols(left, right):
    return lax.dot_general(
        left, right, (((1,), (1,)), ((), ())), preferred_element_type=jnp.float32
    )


def split_heads(matrix, groups):
    row_count = matrix.shape[0]
    return jnp.moveaxis(matrix.reshape(row_count, groups, 2, -1), 1, 0)


def join_heads(stacked):
    row_count = stacked.shape[1]
    return jnp.moveaxis(stacked, 0, 1).reshape(row_count, -1)


def score_block(query_g, key_g, slope_g, distance, allowed):
    scale = 1.0 / math.sqrt(query_g.shape[-1])
    scores = jnp.einsum("qhd,khd->hqk", query_g, key_g, preferred_element_type=jnp.float32) * scale
    scores = scores - slope_g[:, None, None] * distance[None]
    return jnp.where(allowed[None], scores, MASKED)


def group_forward(items, distance, allowed):
    query_g, key_g, value_g, slope_g = items
    scores = score_block(query_g, key_g, slope_g, distance, allowed)
    peak_score = jnp.max(scores, axis=-1, keepdims=True)
    log_total = peak_score + jnp.log(jnp.sum(jnp.exp(scores - peak_score), axis=-1, keepdims=True))
    soft_weights = jnp.exp(scores - log_total).astype(jnp.bfloat16)
    attended = jnp.einsum("hqk,khd->qhd", soft_weights, value_g, preferred_element_type=jnp.float32)
    return (attended, log_total[..., 0])


def group_backward(items, distance, allowed):
    query_g, key_g, value_g, slope_g, log_total, upstream_g = items
    scale = 1.0 / math.sqrt(query_g.shape[-1])
    scores = score_block(query_g, key_g, slope_g, distance, allowed)
    chances = jnp.exp(scores - log_total[..., None])
    soft_weights = chances.astype(jnp.bfloat16)
    soft_grad = jnp.einsum("qhd,khd->hqk", upstream_g, value_g, preferred_element_type=jnp.float32)
    inner_sum = jnp.sum(soft_grad * chances, axis=-1, keepdims=True)
    score_grad = (chances * (soft_grad - inner_sum)).astype(jnp.bfloat16)
    query_grad = (
        jnp.einsum("hqk,khd->qhd", score_grad, key_g, preferred_element_type=jnp.float32) * scale
    ).astype(jnp.bfloat16)
    key_grad = (
        jnp.einsum("hqk,qhd->khd", score_grad, query_g, preferred_element_type=jnp.float32) * scale
    )
    value_grad = jnp.einsum(
        "hqk,qhd->khd", soft_weights, upstream_g, preferred_element_type=jnp.float32
    )
    return (query_grad, key_grad, value_grad)


def on_device(
    tokens,
    cotangent,
    qkv_weight,
    proj_weight,
    up_weight,
    down_weight,
    norm_gains,
    biases,
    up_bias,
    head_slopes,
    qkv_moment,
    proj_moment,
    up_moment,
    down_moment,
    gains_moment,
    biases_moment,
    upbias_moment,
):
    row_count, model_width = tokens.shape
    groups = head_slopes.shape[0] // 2
    seq_length = row_count * lax.axis_size("seq")
    positions = lax.axis_index("seq") * row_count + jnp.arange(row_count, dtype=jnp.int32)
    key_index = jnp.arange(seq_length, dtype=jnp.int32)
    distance = (positions[:, None] - key_index[None, :]).astype(jnp.float32)
    allowed = key_index[None, :] <= positions[:, None]
    slopes = head_slopes.reshape(groups, 2)
    inputs = tokens.astype(jnp.float32)
    normed_one, unit_one, scale_one = norm_forward(inputs, norm_gains[0], biases[0])
    normed_one = normed_one.astype(jnp.bfloat16)
    mixed = jnp.dot(normed_one, qkv_weight, preferred_element_type=jnp.float32)
    queries = (mixed[:, :model_width] + biases[1]).astype(jnp.bfloat16)
    key_part = mixed[:, model_width : 2 * model_width].astype(jnp.bfloat16)
    value_part = (mixed[:, 2 * model_width :] + biases[2]).astype(jnp.bfloat16)
    key_rows, value_rows = (
        lax.all_gather(key_part, "seq", axis=0, tiled=True),
        lax.all_gather(value_part, "seq", axis=0, tiled=True),
    )
    query_groups = split_heads(queries, groups)
    key_groups = split_heads(key_rows, groups)
    value_groups = split_heads(value_rows, groups)

    def forward_group(items):
        return group_forward(items, distance, allowed)

    attended, log_totals = lax.map(forward_group, (query_groups, key_groups, value_groups, slopes))
    mixed_heads = join_heads(attended).astype(jnp.bfloat16)
    middle = (
        inputs + jnp.dot(mixed_heads, proj_weight, preferred_element_type=jnp.float32) + biases[3]
    )
    normed_two, unit_two, scale_two = norm_forward(middle, norm_gains[1], biases[4])
    normed_two = normed_two.astype(jnp.bfloat16)
    before = jnp.dot(normed_two, up_weight, preferred_element_type=jnp.float32) + up_bias
    hidden = gelu_tanh(before).astype(jnp.bfloat16)
    block_out = (
        middle + jnp.dot(hidden, down_weight, preferred_element_type=jnp.float32) + biases[5]
    ).astype(jnp.bfloat16)
    upstream = cotangent.astype(jnp.float32)
    down_grad = contract_rows(cotangent, hidden)
    hidden_grad = contract_cols(cotangent, down_weight)
    before_grad = (hidden_grad * gelu_slope(before)).astype(jnp.bfloat16)
    up_grad = contract_rows(normed_two, before_grad)
    normed_two_grad = contract_cols(before_grad, up_weight)
    middle_back, gain_two_grad, offset_two_grad = norm_backward(
        normed_two_grad, unit_two, scale_two, norm_gains[1]
    )
    middle_grad = upstream + middle_back
    branch_grad = middle_grad.astype(jnp.bfloat16)
    proj_grad = contract_rows(mixed_heads, branch_grad)
    heads_grad = contract_cols(branch_grad, proj_weight).astype(jnp.bfloat16)

    def backward_group(items):
        return group_backward(items, distance, allowed)

    query_grad, key_grad, value_grad = lax.map(
        backward_group,
        (
            query_groups,
            key_groups,
            value_groups,
            slopes,
            log_totals,
            split_heads(heads_grad, groups),
        ),
    )
    query_grad = join_heads(query_grad)
    key_sum, value_sum = (
        lax.psum_scatter(
            join_heads(key_grad).astype(jnp.bfloat16), "seq", scatter_dimension=0, tiled=True
        ).astype(jnp.float32),
        lax.psum_scatter(
            join_heads(value_grad).astype(jnp.bfloat16), "seq", scatter_dimension=0, tiled=True
        ).astype(jnp.float32),
    )
    key_low = key_sum.astype(jnp.bfloat16)
    value_low = value_sum.astype(jnp.bfloat16)
    mixed_grad = jnp.concatenate([query_grad, key_low, value_low], axis=1)
    qkv_grad = contract_rows(normed_one, mixed_grad)
    normed_one_grad = contract_cols(mixed_grad, qkv_weight)
    input_back, gain_one_grad, offset_one_grad = norm_backward(
        normed_one_grad, unit_one, scale_one, norm_gains[0]
    )
    tokens_grad = middle_grad + input_back
    gains_grad = jnp.stack([gain_one_grad, gain_two_grad])
    biases_grad = jnp.stack(
        [
            offset_one_grad,
            jnp.sum(query_grad.astype(jnp.float32), axis=0),
            jnp.sum(value_low.astype(jnp.float32), axis=0),
            jnp.sum(branch_grad.astype(jnp.float32), axis=0),
            offset_two_grad,
            jnp.sum(upstream, axis=0),
        ]
    )
    upbias_grad = jnp.sum(before_grad.astype(jnp.float32), axis=0)[None]
    qkv_part, proj_part, up_part, down_part, gains_part, biases_part, upbias_part = (
        lax.psum_scatter(
            qkv_grad.astype(jnp.bfloat16), "dp", scatter_dimension=1, tiled=True
        ).astype(jnp.float32),
        lax.psum_scatter(
            proj_grad.astype(jnp.bfloat16), "dp", scatter_dimension=1, tiled=True
        ).astype(jnp.float32),
        lax.psum_scatter(
            up_grad.astype(jnp.bfloat16), "dp", scatter_dimension=1, tiled=True
        ).astype(jnp.float32),
        lax.psum_scatter(
            down_grad.astype(jnp.bfloat16), "dp", scatter_dimension=1, tiled=True
        ).astype(jnp.float32),
        lax.psum_scatter(
            gains_grad.astype(jnp.bfloat16), "dp", scatter_dimension=1, tiled=True
        ).astype(jnp.float32),
        lax.psum_scatter(
            biases_grad.astype(jnp.bfloat16), "dp", scatter_dimension=1, tiled=True
        ).astype(jnp.float32),
        lax.psum_scatter(
            upbias_grad.astype(jnp.bfloat16), "dp", scatter_dimension=1, tiled=True
        ).astype(jnp.float32),
    )
    qkv_sum, proj_sum, up_sum, down_sum, gains_sum, biases_sum, upbias_sum = (
        lax.psum(qkv_part.astype(jnp.bfloat16), "seq").astype(jnp.float32),
        lax.psum(proj_part.astype(jnp.bfloat16), "seq").astype(jnp.float32),
        lax.psum(up_part.astype(jnp.bfloat16), "seq").astype(jnp.float32),
        lax.psum(down_part.astype(jnp.bfloat16), "seq").astype(jnp.float32),
        lax.psum(gains_part.astype(jnp.bfloat16), "seq").astype(jnp.float32),
        lax.psum(biases_part.astype(jnp.bfloat16), "seq").astype(jnp.float32),
        lax.psum(upbias_part.astype(jnp.bfloat16), "seq").astype(jnp.float32),
    )
    qkv_state = MOMENTUM * qkv_moment + qkv_sum
    proj_state = MOMENTUM * proj_moment + proj_sum
    up_state = MOMENTUM * up_moment + up_sum
    down_oriented = MOMENTUM * down_moment.T + down_sum
    gains_state = MOMENTUM * gains_moment + gains_sum
    biases_state = MOMENTUM * biases_moment + biases_sum
    upbias_state = MOMENTUM * upbias_moment + upbias_sum[0]
    oriented = (qkv_state, proj_state, up_state, down_oriented)
    pad_width = max((member.shape[1] for member in oriented))
    stacked = jnp.stack(
        [
            jnp.pad(member.astype(jnp.bfloat16), ((0, 0), (0, pad_width - member.shape[1])))
            for member in oriented
        ]
    )
    owned_block = lax.dynamic_index_in_dim(stacked, lax.axis_index("seq"), 0, keepdims=False)
    iterate = owned_block
    for iteration in range(NS_ITERS):
        gram = lax.psum(contract_cols(iterate, iterate).astype(jnp.bfloat16), "dp").astype(
            jnp.float32
        )
        if iteration == 0:
            factor = 1.0 / (jnp.sqrt(jnp.trace(gram)) + ORTHO_EPS)
            square = gram * factor * factor
            iterate = (owned_block.astype(jnp.float32) * factor).astype(jnp.bfloat16)
        else:
            square = gram
        square_low = square.astype(jnp.bfloat16)
        iterate = (
            COEF_A * iterate.astype(jnp.float32)
            + COEF_B * jnp.dot(square_low, iterate, preferred_element_type=jnp.float32)
        ).astype(jnp.bfloat16)
    shared = lax.all_gather(iterate[None], "seq", axis=0, tiled=True)

    def step_of(slot_number, column_count, whole_shape):
        return (
            -RATE_MATRIX
            * math.sqrt(max(whole_shape[0], whole_shape[1]))
            * shared[slot_number][:, :column_count].astype(jnp.float32)
        )

    dp_index = lax.axis_index("dp")

    def own_cols(matrix, count):
        return lax.dynamic_slice_in_dim(matrix, dp_index * count, count, 1).astype(jnp.float32)

    qkv_new = own_cols(qkv_weight, qkv_state.shape[1]) + step_of(
        0, qkv_state.shape[1], qkv_weight.shape
    )
    proj_new = own_cols(proj_weight, proj_state.shape[1]) + step_of(
        1, proj_state.shape[1], proj_weight.shape
    )
    up_new = own_cols(up_weight, up_state.shape[1]) + step_of(2, up_state.shape[1], up_weight.shape)
    down_count = down_oriented.shape[1]
    down_rows = lax.dynamic_slice_in_dim(down_weight, dp_index * down_count, down_count, 0).astype(
        jnp.float32
    )
    down_new = down_rows + step_of(3, down_count, down_weight.shape).T
    gains_new = own_cols(norm_gains, gains_state.shape[1]) - RATE_VECTOR * gains_state
    biases_new = own_cols(biases, biases_state.shape[1]) - RATE_VECTOR * biases_state
    upbias_count = upbias_state.shape[0]
    upbias_new = (
        lax.dynamic_slice_in_dim(up_bias, dp_index * upbias_count, upbias_count, 0)
        - RATE_VECTOR * upbias_state
    )
    return (
        block_out,
        tokens_grad,
        qkv_sum,
        proj_sum,
        up_sum,
        down_sum.T,
        gains_sum,
        biases_sum,
        upbias_sum[0],
        qkv_state,
        proj_state,
        up_state,
        down_oriented.T,
        gains_state,
        biases_state,
        upbias_state,
        qkv_new,
        proj_new,
        up_new,
        down_new,
        gains_new,
        biases_new,
        upbias_new,
    )


def solution(mesh):
    placed = (
        P(("dp", "seq"), None),
        P(("dp", "seq"), None),
        P(),
        P(),
        P(),
        P(),
        P(),
        P(),
        P(),
        P(),
        P(None, "dp"),
        P(None, "dp"),
        P(None, "dp"),
        P("dp", None),
        P(None, "dp"),
        P(None, "dp"),
        P("dp"),
    )
    return jax.shard_map(
        on_device,
        mesh=mesh,
        in_specs=placed,
        out_specs=(
            P(("dp", "seq"), None),
            P(("dp", "seq"), None),
            P(None, "dp"),
            P(None, "dp"),
            P(None, "dp"),
            P("dp", None),
            P(None, "dp"),
            P(None, "dp"),
            P("dp"),
            P(None, "dp"),
            P(None, "dp"),
            P(None, "dp"),
            P("dp", None),
            P(None, "dp"),
            P(None, "dp"),
            P("dp"),
            P(None, "dp"),
            P(None, "dp"),
            P(None, "dp"),
            P("dp", None),
            P(None, "dp"),
            P(None, "dp"),
            P("dp"),
        ),
        check_vma=False,
    )
```

profile of v0, /device:TPU:0, one launch (start us, length us, event | category | flops | bytes accessed | tf_op | source)
XLA Modules:
  0.0 1661.3 jit_solution(17056713743389701598)
XLA Ops:
  12.8 6.1 fusion.105
  26.7 78.8 %all-gather.5.cloned.1.call-done = bf16[2048,1024]{1,0:T(8,128)(2,1)} async-done(((bf16[512,1024]{1,0:T(8,128)(2,1)}), bf16[2048,1024]{1,0:T(8,128)(2,1)}) %all-gather.5.cloned.1.call-update) | async-done | bytes 4194320 | tf_op jit(solution)/shard_map/all_gather | solution.py:142
  105.5 6.5 copy.60
  112.0 74.9 %all-gather.7.cloned.1.call-done = bf16[2048,1024]{1,0:T(8,128)(2,1)} async-done(((bf16[512,1024]{1,0:T(8,128)(2,1)}), bf16[2048,1024]{1,0:T(8,128)(2,1)}) %all-gather.7.cloned.1.call-update) | async-done | bytes 4194320 | tf_op jit(solution)/shard_map/all_gather | solution.py:141
  186.9 6.5 copy.62
  193.4 102.7 %while.30 = (s32[]{:T(128)}, bf16[8,512,2,64]{1,3,2,0:T(8,128)(2,1)}, f32[8,2,512]{2,1,0:T(2,128)S(1)}, bf16[8,2048,2,64]{1,3,2,0:T(8,128)(2,1)}, bf16[8,512,2,6...) while((s32[]{:T(128)}, ...), condition=%wide.region_5.6_spmd.clone.clone, body=%wide.region_2.5_spmd.clone.clone.sunk | while | flops 575667200 | bytes 47618196 | solution.py:151
  201.7 4.5 fusion.167
  214.5 4.5 fusion.167
  220.1 4.0 fusion.166
  227.4 4.5 fusion.167
  240.2 4.5 fusion.167
  253.0 4.5 fusion.167
  265.9 4.5 fusion.167
  278.7 4.5 fusion.167
  291.5 4.5 fusion.167
  299.1 10.7 fusion.107
  309.8 13.6 fusion.113
  323.4 5.7 multiply_reduce_fusion.1
  334.6 222.8 %while.31 = (s32[]{:T(128)}, bf16[8,512,2,64]{1,3,2,0:T(8,128)(2,1)}, bf16[8,2048,2,64]{1,3,2,0:T(8,128)(2,1)}, bf16[8,2048,2,64]{1,3,2,0:T(8,128)(2,1)}, bf16[8...) while((s32[]{:T(128)}, ...), condition=%wide.region_12.13_spmd.clone.clone, body=%wide.region_10.12_spmd.clone.clone.sunk | while | flops 1368783872 | bytes 144864496 | solution.py:180
  343.3 5.7 multiply_reduce_fusion.7
  349.0 6.6 multiply_convert_fusion.7
  371.1 5.7 multiply_reduce_fusion.7
  376.8 6.6 multiply_convert_fusion.7
  391.5 4.0 subtract_exponential_fusion.2
  398.9 5.7 multiply_reduce_fusion.7
  404.6 6.6 multiply_convert_fusion.7
  419.3 4.0 subtract_exponential_fusion.2
  426.7 5.7 multiply_reduce_fusion.7
  432.4 6.6 multiply_convert_fusion.7
  454.5 5.7 multiply_reduce_fusion.7
  460.3 6.6 multiply_convert_fusion.7
  482.4 5.7 multiply_reduce_fusion.7
  488.1 6.6 multiply_convert_fusion.7
  510.2 5.7 multiply_reduce_fusion.7
  515.9 6.6 multiply_convert_fusion.7
  530.6 4.0 subtract_exponential_fusion.2
  538.0 5.7 multiply_reduce_fusion.7
  543.7 6.6 multiply_convert_fusion.7
  561.8 4.3 copy.73
  566.6 66.1 %reduce-scatter.20.cloned.1.call-done = bf16[512,1024]{0,1:T(8,128)(2,1)} async-done(((bf16[2048,1024]{0,1:T(8,128)(2,1)}), bf16[512,1024]{0,1:T(8,128)(2,1)}) %reduce-scatter.20.cloned.1.call-update) | async-done | bytes 1048592 | tf_op jit(solution)/shard_map/reduce_scatter | solution.py:193
  632.7 79.5 %reduce-scatter.22.cloned.1.call-done = bf16[512,1024]{0,1:T(8,128)(2,1)} async-done(((bf16[2048,1024]{0,1:T(8,128)(2,1)}), bf16[512,1024]{0,1:T(8,128)(2,1)}) %reduce-scatter.22.cloned.1.call-update) | async-done | bytes 1048592 | tf_op jit(solution)/shard_map/reduce_scatter | solution.py:196
  712.2 8.1 convolution_convert_fusion.1
  720.3 8.6 copy.71
  730.2 11.4 convert_bitcast_fusion
  743.2 9.2 convolution_convert_fusion
  752.7 4.9 reduce-scatter.30.cloned.1.call-done
  759.4 63.2 %reduce-scatter.28.cloned.1.call-done = bf16[384,1024]{1,0:T(8,128)(2,1)} async-done(((bf16[3072,1024]{1,0:T(8,128)(2,1)}), bf16[384,1024]{1,0:T(8,128)(2,1)}) %reduce-scatter.28.cloned.1.call-update) | async-done | bytes 786448
  824.9 72.5 %reduce-scatter.26.cloned.1.call-done = bf16[1024,512]{1,0:T(8,128)(2,1)} async-done(((bf16[1024,4096]{1,0:T(8,128)(2,1)}), bf16[1024,512]{1,0:T(8,128)(2,1)}) %reduce-scatter.26.cloned.1.call-update) | async-done | bytes 1048592 | tf_op jit(solution)/shard_map/reduce_scatter | solution.py:231
  897.4 74.8 %reduce-scatter.24.cloned.1.call-done = bf16[1024,512]{1,0:T(8,128)(2,1)} async-done(((bf16[1024,4096]{1,0:T(8,128)(2,1)}), bf16[1024,512]{1,0:T(8,128)(2,1)}) %reduce-scatter.24.cloned.1.call-update) | async-done | bytes 1048592 | tf_op jit(solution)/shard_map/reduce_scatter | solution.py:228
  975.1 121.9 %all-reduce.21.cloned.1.call-done = (bf16[1024,384]{1,0:T(8,128)(2,1)}, bf16[1024,128]{1,0:T(8,128)(2,1)}, bf16[1024,512]{1,0:T(8,128)(2,1)}, bf16[1024,512]{1,0:T(8,128)(2,1)}) async-done(((bf16[1024,384]{1,0:T(8,128)(2,1)}, bf16[1024,128]{1,0:T(8,128)(2,1)}, bf16[1024,512]{1,0:T(8,128)(2,1)}, bf16[1024,512]{1,0:T(8,128)(2,1)}), (bf16[1024,384]{1,0:T(8,128)(2,1)}, bf16[1024,128]{1,0:T(8,128)(2,1)}, ...) | async-done | bytes 3145744 | tf_op jit(solution)/shard_map/psum | solution.py:245
  1112.3 60.9 %all-reduce.11.cloned.1.call-done = bf16[1024,1024]{1,0:T(8,128)(2,1)} async-done(((bf16[1024,1024]{1,0:T(8,128)(2,1)}), bf16[1024,1024]{1,0:T(8,128)(2,1)}) %all-reduce.11.cloned.1.call-update) | async-done | bytes 2097168 | tf_op jit(solution)/shard_map/psum | solution.py:271
  1183.4 60.9 %all-reduce.13.cloned.1.call-done = bf16[1024,1024]{1,0:T(8,128)(2,1)} async-done(((bf16[1024,1024]{1,0:T(8,128)(2,1)}), bf16[1024,1024]{1,0:T(8,128)(2,1)}) %all-reduce.13.cloned.1.call-update) | async-done | bytes 2097168 | tf_op jit(solution)/shard_map/psum | solution.py:271
  1251.4 60.9 %all-reduce.15.cloned.1.call-done = bf16[1024,1024]{1,0:T(8,128)(2,1)} async-done(((bf16[1024,1024]{1,0:T(8,128)(2,1)}), bf16[1024,1024]{1,0:T(8,128)(2,1)}) %all-reduce.15.cloned.1.call-update) | async-done | bytes 2097168 | tf_op jit(solution)/shard_map/psum | solution.py:271
  1319.5 60.9 %all-reduce.17.cloned.1.call-done = bf16[1024,1024]{1,0:T(8,128)(2,1)} async-done(((bf16[1024,1024]{1,0:T(8,128)(2,1)}), bf16[1024,1024]{1,0:T(8,128)(2,1)}) %all-reduce.17.cloned.1.call-update) | async-done | bytes 2097168 | tf_op jit(solution)/shard_map/psum | solution.py:271
  1389.4 9.4 fusion.80
  1404.0 44.5 %all-reduce.19.cloned.1.call-done = bf16[1024,1024]{1,0:T(8,128)(2,1)} async-done(((bf16[1024,1024]{1,0:T(8,128)(2,1)}), bf16[1024,1024]{1,0:T(8,128)(2,1)}) %all-reduce.19.cloned.1.call-update) | async-done | bytes 2097168 | tf_op jit(solution)/shard_map/psum | solution.py:271
  1448.5 4.4 add_convert_fusion
  1457.5 12.6 add_convert_fusion.5
  1470.1 17.1 %reduce-scatter.36.cloned.1.call-done = bf16[512,1]{1,0:T(8,128)(2,1)} async-done(((bf16[4096,1]{1,0:T(8,128)(2,1)}), bf16[512,1]{1,0:T(8,128)(2,1)}) %reduce-scatter.36.cloned.1.call-update) | async-done | bytes 1040
  1488.3 4.2 fusion.79
  1492.5 31.8 %reduce-scatter.32.cloned.1.call-done = bf16[128,2]{1,0:T(8,128)(2,1)} async-done(((bf16[1024,2]{1,0:T(8,128)(2,1)}), bf16[128,2]{1,0:T(8,128)(2,1)}) %reduce-scatter.32.cloned.1.call-update) | async-done | bytes 528
  1525.2 35.7 %reduce-scatter.34.cloned.1.call-done = bf16[128,6]{1,0:T(8,128)(2,1)} async-done(((bf16[1024,6]{1,0:T(8,128)(2,1)}), bf16[128,6]{1,0:T(8,128)(2,1)}) %reduce-scatter.34.cloned.1.call-update) | async-done | bytes 1552
  1561.7 11.8 all-reduce.2
  1584.4 58.7 %all-gather.9.cloned.1.call-done = bf16[4096,512]{1,0:T(8,128)(2,1)} async-done(((bf16[1024,512]{1,0:T(8,128)(2,1)}), bf16[4096,512]{1,0:T(8,128)(2,1)}) %all-gather.9.cloned.1.call-update) | async-done | bytes 4194320 | tf_op jit(solution)/shard_map/all_gather | solution.py:285
  (369 shorter events, 292.4 us)
Async XLA Ops:
  7.2 98.3 %all-gather.5.cloned.1.call-start = ((), (), s32[]{:S(2)}) async-start(), calls=%async_computation.9 | async-start | bytes 5242880 | tf_op jit(solution)/shard_map/all_gather | solution.py:142
  8.7 10.2 copy-start.24
  10.3 8.5 copy-start.31
  11.1 7.7 copy-start.26
  12.7 6.1 copy-start.36
  12.8 286.3 %copy-start.34 = (f32[1,1024]{1,0:T(1,128)}, f32[1,1024]{1,0:T(1,128)S(1)}, u32[]{:S(2)}) copy-start(f32[1,1024]{1,0:T(1,128)S(1)} %get-tuple-element.393) | copy-start | bytes 12292
  21.8 3.4 copy-start.43
  21.9 165.0 %all-gather.7.cloned.1.call-start = ((), (), s32[]{:S(2)}) async-start(), calls=%async_computation.10 | async-start | bytes 5242880 | tf_op jit(solution)/shard_map/all_gather | solution.py:141
  24.7 608.1 %reduce-scatter.20.cloned.1.call-start = ((), (), s32[]{:S(2)}) async-start(), calls=%async_computation.11 | async-start | bytes 5242880 | tf_op jit(solution)/shard_map/reduce_scatter | solution.py:193
  193.4 102.7 %copy-start.3 = (bf16[512,1024]{1,0:T(8,128)(2,1)S(1)}, bf16[512,1024]{1,0:T(8,128)(2,1)}, u32[]{:S(2)}) copy-start(bf16[512,1024]{1,0:T(8,128)(2,1)} %param.21) | copy-start | bytes 3145732
  193.4 102.7 %copy-start.14 = (bf16[1024,1024]{1,0:T(8,128)(2,1)S(1)}, bf16[1024,1024]{1,0:T(8,128)(2,1)}, u32[]{:S(2)}) copy-start(bf16[1024,1024]{1,0:T(8,128)(2,1)} %param.24) | copy-start | bytes 6291460
  298.6 30.4 %copy-start.1 = (f32[512,1024]{1,0:T(8,128)}, f32[512,1024]{1,0:T(8,128)S(1)}, u32[]{:S(2)}) copy-start(f32[512,1024]{1,0:T(8,128)S(1)} %get-tuple-element.402) | copy-start | bytes 6291460
  299.0 10.8 copy-start.17
  299.0 10.8 copy-start.44
  299.0 24.3 %slice-start = ((s8[8388608]{0:T(1024)(128)(4,1)}), s8[4194304]{0:T(1024)(128)(4,1)S(1)}, s32[]{:S(2)}) async-start(s8[8388608]{0:T(1024)(128)(4,1)} %bitcast.226), calls=%async_computation.27 | async-start | bytes 8388608
  309.8 13.6 slice-start.1
  323.4 5.7 copy-start.49
  339.9 3.4 copy-start
  355.6 3.3 copy-start.10
  367.7 3.4 copy-start
  383.4 3.3 copy-start.10
  395.5 3.4 copy-start
  411.2 3.3 copy-start.10
  423.3 3.4 copy-start
  439.0 3.3 copy-start.10
  451.1 3.4 copy-start
  466.8 3.3 copy-start.10
  478.9 3.4 copy-start
  494.7 3.3 copy-start.10
  506.8 3.4 copy-start
  522.5 3.3 copy-start.10
  534.6 3.4 copy-start
  550.3 3.3 copy-start.10
  557.4 154.8 %reduce-scatter.22.cloned.1.call-start = ((), (), s32[]{:S(2)}) async-start(), calls=%async_computation.12 | async-start | bytes 5242880 | tf_op jit(solution)/shard_map/reduce_scatter | solution.py:196
  558.0 199.6 %reduce-scatter.30.cloned.1.call-start = ((), (), s32[]{:S(2)}) async-start(), calls=%async_computation.22 | async-start | bytes 2359296
  561.8 150.4 %copy-start.4 = (bf16[512,1024]{1,0:T(8,128)(2,1)S(1)}, bf16[512,1024]{1,0:T(8,128)(2,1)}, u32[]{:S(2)}) copy-start(bf16[512,1024]{1,0:T(8,128)(2,1)} %param.21) | copy-start | bytes 3145732
  561.8 150.4 %copy-start.19 = (bf16[8,512,2,64]{1,3,2,0:T(8,128)(2,1)S(1)}, bf16[8,512,2,64]{1,3,2,0:T(8,128)(2,1)}, u32[]{:S(2)}) copy-start(bf16[8,512,2,64]{1,3,2,0:T(8,128)(2,1)} %get-tuple-element.137) | copy-start | bytes 3145732
  561.8 150.4 %copy-start.25 = (f32[512]{0:T(512)S(1)}, f32[512]{0:T(512)}, u32[]{:S(2)}) copy-start(f32[512]{0:T(512)} %copy-done.24) | copy-start | bytes 6148
  561.8 150.4 %copy-start.27 = (f32[1,1024]{1,0:T(1,128)S(1)}, f32[1,1024]{1,0:T(1,128)}, u32[]{:S(2)}) copy-start(f32[1,1024]{1,0:T(1,128)} %copy-done.26) | copy-start | bytes 12292
  561.8 150.4 %copy-start.32 = (f32[512]{0:T(512)S(1)}, f32[512]{0:T(512)}, u32[]{:S(2)}) copy-start(f32[512]{0:T(512)} %copy-done.31) | copy-start | bytes 6148
  561.8 150.4 %copy-start.37 = (f32[1,1024]{1,0:T(1,128)S(1)}, f32[1,1024]{1,0:T(1,128)}, u32[]{:S(2)}) copy-start(f32[1,1024]{1,0:T(1,128)} %copy-done.36) | copy-start | bytes 12292
  566.1 256.4 %reduce-scatter.28.cloned.1.call-start = ((), (), s32[]{:S(2)}) async-start(), calls=%async_computation.21 | async-start | bytes 7077888
  729.0 168.4 %reduce-scatter.26.cloned.1.call-start = ((), (), s32[]{:S(2)}) async-start(), calls=%async_computation.14 | async-start | bytes 9437184 | tf_op jit(solution)/shard_map/reduce_scatter | solution.py:231
  741.6 230.6 %reduce-scatter.24.cloned.1.call-start = ((), (), s32[]{:S(2)}) async-start(), calls=%async_computation.13 | async-start | bytes 9437184 | tf_op jit(solution)/shard_map/reduce_scatter | solution.py:228
  752.5 344.6 %all-reduce.21.cloned.1.call-start = ((), (), s32[]{:S(2)}) async-start(), calls=%async_computation.26 | async-start | bytes 6291456 | tf_op jit(solution)/shard_map/psum | solution.py:245
  972.2 200.9 %all-reduce.11.cloned.1.call-start = ((), (), s32[]{:S(2)}) async-start(), calls=%async_computation.15 | async-start | bytes 4194304 | tf_op jit(solution)/shard_map/psum | solution.py:271
  1099.5 3.0 copy-start.12
  1112.2 132.2 %all-reduce.13.cloned.1.call-start = ((), (), s32[]{:S(2)}) async-start(), calls=%async_computation.16 | async-start | bytes 4194304 | tf_op jit(solution)/shard_map/psum | solution.py:271
  1183.4 129.0 %all-reduce.15.cloned.1.call-start = ((), (), s32[]{:S(2)}) async-start(), calls=%async_computation.17 | async-start | bytes 4194304 | tf_op jit(solution)/shard_map/psum | solution.py:271
  1251.4 129.0 %all-reduce.17.cloned.1.call-start = ((), (), s32[]{:S(2)}) async-start(), calls=%async_computation.18 | async-start | bytes 4194304 | tf_op jit(solution)/shard_map/psum | solution.py:271
  1319.4 129.1 %all-reduce.19.cloned.1.call-start = ((), (), s32[]{:S(2)}) async-start(), calls=%async_computation.19 | async-start | bytes 4194304 | tf_op jit(solution)/shard_map/psum | solution.py:271
  1387.5 99.7 %reduce-scatter.36.cloned.1.call-start = ((), (), s32[]{:S(2)}) async-start(), calls=%async_computation.25 | async-start | bytes 1179648
  1389.1 12.2 copy-start.39
  1389.2 12.2 copy-start.30
  1389.2 12.2 copy-start.29
  1389.2 135.2 %reduce-scatter.32.cloned.1.call-start = ((), (), s32[]{:S(2)}) async-start(), calls=%async_computation.23 | async-start | bytes 294912
  1399.8 161.1 %reduce-scatter.34.cloned.1.call-start = ((), (), s32[]{:S(2)}) async-start(), calls=%async_computation.24 | async-start | bytes 294912
  1403.9 239.2 %all-gather.9.cloned.1.call-start = ((), (), s32[]{:S(2)}) async-start(), calls=%async_computation.20 | async-start | bytes 5242880 | tf_op jit(solution)/shard_map/all_gather | solution.py:285
  1452.9 4.6 copy-start.33
  1488.2 85.3 %copy-start.42 = (f32[2,128]{1,0:T(2,128)S(1)}, f32[2,128]{1,0:T(2,128)}, u32[]{:S(2)}) copy-start(f32[2,128]{1,0:T(2,128)} %param.35) | copy-start | bytes 3076
  1488.2 86.5 %copy-start.41 = (f32[512]{0:T(512)S(1)}, f32[512]{0:T(512)}, u32[]{:S(2)}) copy-start(f32[512]{0:T(512)} %param.37) | copy-start | bytes 6148
  1488.3 87.2 %copy-start.38 = (f32[6,128]{1,0:T(8,128)S(1)}, f32[6,128]{1,0:T(8,128)}, u32[]{:S(2)}) copy-start(f32[6,128]{1,0:T(8,128)} %param.36) | copy-start | bytes 9220
  1576.7 5.9 copy-start.5
  1582.6 60.5 %copy-start.13 = (bf16[512,1024]{0,1:T(8,128)(2,1)S(1)}, bf16[512,1024]{0,1:T(8,128)(2,1)}, u32[]{:S(2)}) copy-start(bf16[512,1024]{0,1:T(8,128)(2,1)} %copy.81) | copy-start | bytes 3145732
  (27 other events, 50.7 us)
Sparse Core Ops, SparseCore 0:
  22.0 83.4 all-gather.4
  107.6 79.2 all-gather.6
  557.5 75.1 reduce-scatter.19
  634.9 77.2 reduce-scatter.21
  715.9 41.6 reduce-scatter.29
  760.8 61.7 reduce-scatter.27
  826.0 71.3 reduce-scatter.25
  900.9 71.2 reduce-scatter.23
  976.0 121.0 all-reduce.20
  1112.3 60.7 all-reduce.10
  1183.5 60.8 all-reduce.12
  1251.5 60.8 all-reduce.14
  1319.6 60.8 all-reduce.16
  1387.6 60.8 all-reduce.18
  1452.1 35.0 reduce-scatter.35
  1490.6 33.6 reduce-scatter.31
  1527.2 33.6 reduce-scatter.33
  1562.3 80.7 all-gather.8
where the time goes:
time: 1670 us; the launch traced here: 1660 us
  waiting for transfers between devices  1070 us (64%)
  matrix products  337 us (20%)
  other arithmetic  136 us (8%)
  local copies, waits for them, and re-layouts  88.3 us (5%)
    psum x5, waiting for transfers between devices, on_device(): lax.psum(contract_cols(iterate, iterate).astype(jnp.bfloat16), 'dp')  288 us
    unnamed x23, waiting for transfers between devices  154 us
    psum x1, waiting for transfers between devices, on_device(): lax.psum(qkv_part.astype(jnp.bfloat16), 'seq').astype(jnp.float32)  122 us
    reduce_scatter x1, waiting for transfers between devices, on_device(): lax.psum_scatter(join_heads(value_grad).astype(jnp.bfloat16), 'seq', scat...  79.5 us
    all_gather x1, waiting for transfers between devices, on_device(): lax.all_gather(value_part, 'seq', axis=0, tiled=True)  78.8 us
    all_gather x1, waiting for transfers between devices, on_device(): lax.all_gather(key_part, 'seq', axis=0, tiled=True)  74.9 us
    reduce_scatter x1, waiting for transfers between devices, on_device(): lax.psum_scatter(up_grad.astype(jnp.bfloat16), 'dp', scatter_dimension=1,...  74.8 us
    reduce_scatter x1, waiting for transfers between devices, on_device(): lax.psum_scatter(down_grad.astype(jnp.bfloat16), 'dp', scatter_dimension=...  72.5 us
  transfers between devices with their start and end apart: 18, of which 18 were waited for; matrix products, arithmetic and copies ran while one was open for 7% of the time, Pallas kernels for 0%

commit v1 on v0

--- a/solution.py
+++ b/solution.py
@@ -268,9 +268,9 @@
     owned_block = lax.dynamic_index_in_dim(stacked, lax.axis_index("seq"), 0, keepdims=False)
     iterate = owned_block
     for iteration in range(NS_ITERS):
-        gram = lax.psum(contract_cols(iterate, iterate).astype(jnp.bfloat16), "dp").astype(
-            jnp.float32
-        )
+        gram = jnp.sum(
+            lax.all_gather(contract_cols(iterate, iterate).astype(jnp.bfloat16), "dp"), axis=0
+        ).astype(jnp.float32)
         if iteration == 0:
             factor = 1.0 / (jnp.sqrt(jnp.trace(gram)) + ORTHO_EPS)
             square = gram * factor * factor

time: 1670 us -> 1860 us (1.11)
  waiting for transfers between devices: 1070 us -> 1200 us
  other arithmetic: 136 us -> 190 us
    all_gather x0 -> x5, waiting for transfers between devices: none -> 432 us  [on_device(): lax.all_gather(contract_cols(iterate, iterate).astype(jnp.bfloat16), 'dp')]
    psum x5 -> x0, waiting for transfers between devices: 288 us -> none  [on_device(): lax.psum(contract_cols(iterate, iterate).astype(jnp.bfloat16), 'dp')]
    reduce_sum x0 -> x5, other arithmetic: none -> 53.9 us  [on_device(): jnp.sum(lax.all_gather(contract_cols(iterate, iterate).astype(jnp.bfloat1...]
    unnamed x112 -> x110, local copies, waits for them, and re-layouts: 46.7 us -> 47.4 us
where the time goes in v1:
time: 1860 us; the launch traced here: 1850 us
  waiting for transfers between devices  1200 us (65%)
  matrix products  337 us (18%)
  other arithmetic  190 us (10%)
  local copies, waits for them, and re-layouts  89.1 us (5%)
    all_gather x5, waiting for transfers between devices, on_device(): lax.all_gather(contract_cols(iterate, iterate).astype(jnp.bfloat16), 'dp')  432 us
    unnamed x23, waiting for transfers between devices  144 us
    psum x1, waiting for transfers between devices, on_device(): lax.psum(qkv_part.astype(jnp.bfloat16), 'seq').astype(jnp.float32)  122 us
    reduce_scatter x1, waiting for transfers between devices, on_device(): lax.psum_scatter(join_heads(value_grad).astype(jnp.bfloat16), 'seq', scat...  79.5 us
    all_gather x1, waiting for transfers between devices, on_device(): lax.all_gather(value_part, 'seq', axis=0, tiled=True)  79 us
    all_gather x1, waiting for transfers between devices, on_device(): lax.all_gather(key_part, 'seq', axis=0, tiled=True)  74.9 us
    reduce_scatter x1, waiting for transfers between devices, on_device(): lax.psum_scatter(up_grad.astype(jnp.bfloat16), 'dp', scatter_dimension=1,...  74.8 us
    reduce_scatter x1, waiting for transfers between devices, on_device(): lax.psum_scatter(down_grad.astype(jnp.bfloat16), 'dp', scatter_dimension=...  72.5 us
  transfers between devices with their start and end apart: 18, of which 18 were waited for; matrix products, arithmetic and copies ran while one was open for 7% of the time, Pallas kernels for 0%

profile of v1, /device:TPU:0, one launch (start us, length us, event | category | flops | bytes accessed | tf_op | source)
XLA Modules:
  0.0 1850.7 jit_solution(11213855683567013093)
XLA Ops:
  12.8 6.1 fusion.105
  27.7 79.0 %all-gather.15.cloned.1.call-done = bf16[2048,1024]{1,0:T(8,128)(2,1)} async-done(((bf16[512,1024]{1,0:T(8,128)(2,1)}), bf16[2048,1024]{1,0:T(8,128)(2,1)}) %all-gather.15.cloned.1.call-update) | async-done | bytes 4194320 | tf_op jit(solution)/shard_map/all_gather | solution.py:142
  106.7 6.5 copy.70
  113.2 74.9 %all-gather.17.cloned.1.call-done = bf16[2048,1024]{1,0:T(8,128)(2,1)} async-done(((bf16[512,1024]{1,0:T(8,128)(2,1)}), bf16[2048,1024]{1,0:T(8,128)(2,1)}) %all-gather.17.cloned.1.call-update) | async-done | bytes 4194320 | tf_op jit(solution)/shard_map/all_gather | solution.py:141
  188.1 6.4 copy.72
  194.6 102.7 %while.30 = (s32[]{:T(128)}, bf16[8,512,2,64]{1,3,2,0:T(8,128)(2,1)}, f32[8,2,512]{2,1,0:T(2,128)S(1)}, bf16[8,2048,2,64]{1,3,2,0:T(8,128)(2,1)}, bf16[8,512,2,6...) while((s32[]{:T(128)}, ...), condition=%wide.region_5.6_spmd.clone.clone, body=%wide.region_2.5_spmd.clone.clone.sunk | while | flops 575667200 | bytes 47618196 | solution.py:151
  202.9 4.5 fusion.167
  215.7 4.5 fusion.167
  228.6 4.5 fusion.167
  241.4 4.5 fusion.167
  254.2 4.5 fusion.167
  267.1 4.5 fusion.167
  279.9 4.5 fusion.167
  292.7 4.5 fusion.167
  300.3 10.7 fusion.107
  311.0 14.0 fusion.113
  325.0 5.7 multiply_reduce_fusion.1
  336.3 222.9 %while.31 = (s32[]{:T(128)}, bf16[8,512,2,64]{1,3,2,0:T(8,128)(2,1)}, bf16[8,2048,2,64]{1,3,2,0:T(8,128)(2,1)}, bf16[8,2048,2,64]{1,3,2,0:T(8,128)(2,1)}, bf16[8...) while((s32[]{:T(128)}, ...), condition=%wide.region_12.13_spmd.clone.clone, body=%wide.region_10.12_spmd.clone.clone.sunk | while | flops 1368783872 | bytes 144864496 | solution.py:180
  344.9 5.7 multiply_reduce_fusion.7
  350.6 6.6 multiply_convert_fusion.7
  372.7 5.7 multiply_reduce_fusion.7
  378.5 6.6 multiply_convert_fusion.7
  400.6 5.7 multiply_reduce_fusion.7
  406.3 6.6 multiply_convert_fusion.7
  428.4 5.7 multiply_reduce_fusion.7
  434.1 6.6 multiply_convert_fusion.7
  456.3 5.7 multiply_reduce_fusion.7
  462.0 6.6 multiply_convert_fusion.7
  484.1 5.7 multiply_reduce_fusion.7
  489.8 6.6 multiply_convert_fusion.7
  512.0 5.7 multiply_reduce_fusion.7
  517.7 6.6 multiply_convert_fusion.7
  539.8 5.7 multiply_reduce_fusion.7
  545.5 6.6 multiply_convert_fusion.7
  563.6 4.3 copy.83
  568.2 66.4 %reduce-scatter.20.cloned.1.call-done = bf16[512,1024]{0,1:T(8,128)(2,1)} async-done(((bf16[2048,1024]{0,1:T(8,128)(2,1)}), bf16[512,1024]{0,1:T(8,128)(2,1)}) %reduce-scatter.20.cloned.1.call-update) | async-done | bytes 1048592 | tf_op jit(solution)/shard_map/reduce_scatter | solution.py:193
  634.5 79.5 %reduce-scatter.22.cloned.1.call-done = bf16[512,1024]{0,1:T(8,128)(2,1)} async-done(((bf16[2048,1024]{0,1:T(8,128)(2,1)}), bf16[512,1024]{0,1:T(8,128)(2,1)}) %reduce-scatter.22.cloned.1.call-update) | async-done | bytes 1048592 | tf_op jit(solution)/shard_map/reduce_scatter | solution.py:196
  714.1 8.0 convolution_convert_fusion.1
  722.1 8.7 copy.81
  732.0 11.4 convert_bitcast_fusion
  745.0 9.2 convolution_convert_fusion
  754.7 4.7 reduce-scatter.30.cloned.1.call-done
  761.2 63.2 %reduce-scatter.28.cloned.1.call-done = bf16[384,1024]{1,0:T(8,128)(2,1)} async-done(((bf16[3072,1024]{1,0:T(8,128)(2,1)}), bf16[384,1024]{1,0:T(8,128)(2,1)}) %reduce-scatter.28.cloned.1.call-update) | async-done | bytes 786448
  826.6 72.5 %reduce-scatter.26.cloned.1.call-done = bf16[1024,512]{1,0:T(8,128)(2,1)} async-done(((bf16[1024,4096]{1,0:T(8,128)(2,1)}), bf16[1024,512]{1,0:T(8,128)(2,1)}) %reduce-scatter.26.cloned.1.call-update) | async-done | bytes 1048592 | tf_op jit(solution)/shard_map/reduce_scatter | solution.py:231
  899.2 74.8 %reduce-scatter.24.cloned.1.call-done = bf16[1024,512]{1,0:T(8,128)(2,1)} async-done(((bf16[1024,4096]{1,0:T(8,128)(2,1)}), bf16[1024,512]{1,0:T(8,128)(2,1)}) %reduce-scatter.24.cloned.1.call-update) | async-done | bytes 1048592 | tf_op jit(solution)/shard_map/reduce_scatter | solution.py:228
  976.9 121.9 %all-reduce.6.cloned.1.call-done = (bf16[1024,384]{1,0:T(8,128)(2,1)}, bf16[1024,128]{1,0:T(8,128)(2,1)}, bf16[1024,512]{1,0:T(8,128)(2,1)}, bf16[1024,512]{1,0:T(8,128)(2,1)}) async-done(((bf16[1024,384]{1,0:T(8,128)(2,1)}, bf16[1024,128]{1,0:T(8,128)(2,1)}, bf16[1024,512]{1,0:T(8,128)(2,1)}, bf16[1024,512]{1,0:T(8,128)(2,1)}), (bf16[1024,384]{1,0:T(8,128)(2,1)}, bf16[1024,128]{1,0:T(8,128)(2,1)}, ...) | async-done | bytes 3145744 | tf_op jit(solution)/shard_map/psum | solution.py:245
  1114.2 88.8 %all-gather.19.cloned.1.call-done = bf16[8192,1024]{1,0:T(8,128)(2,1)} async-done(((bf16[1024,1024]{1,0:T(8,128)(2,1)}), bf16[8192,1024]{1,0:T(8,128)(2,1)}) %all-gather.19.cloned.1.call-update) | async-done | bytes 16777232 | tf_op jit(solution)/shard_map/all_gather | solution.py:272
  1203.1 10.8 reduce_sum.261
  1224.1 89.8 %all-gather.21.cloned.1.call-done = bf16[8192,1024]{1,0:T(8,128)(2,1)} async-done(((bf16[1024,1024]{1,0:T(8,128)(2,1)}), bf16[8192,1024]{1,0:T(8,128)(2,1)}) %all-gather.21.cloned.1.call-update) | async-done | bytes 16777232 | tf_op jit(solution)/shard_map/all_gather | solution.py:272
  1314.0 10.8 reduce_sum.263
  1332.0 89.6 %all-gather.23.cloned.1.call-done = bf16[8192,1024]{1,0:T(8,128)(2,1)} async-done(((bf16[1024,1024]{1,0:T(8,128)(2,1)}), bf16[8192,1024]{1,0:T(8,128)(2,1)}) %all-gather.23.cloned.1.call-update) | async-done | bytes 16777232 | tf_op jit(solution)/shard_map/all_gather | solution.py:272
  1421.6 10.8 reduce_sum.264
  1439.5 89.8 %all-gather.25.cloned.1.call-done = bf16[8192,1024]{1,0:T(8,128)(2,1)} async-done(((bf16[1024,1024]{1,0:T(8,128)(2,1)}), bf16[8192,1024]{1,0:T(8,128)(2,1)}) %all-gather.25.cloned.1.call-update) | async-done | bytes 16777232 | tf_op jit(solution)/shard_map/all_gather | solution.py:272
  1529.3 10.8 reduce_sum.265
  1548.9 9.0 fusion.80
  1563.3 73.8 %all-gather.27.cloned.1.call-done = bf16[8192,1024]{1,0:T(8,128)(2,1)} async-done(((bf16[1024,1024]{1,0:T(8,128)(2,1)}), bf16[8192,1024]{1,0:T(8,128)(2,1)}) %all-gather.27.cloned.1.call-update) | async-done | bytes 16777232 | tf_op jit(solution)/shard_map/all_gather | solution.py:272
  1637.0 10.8 reduce_sum.266
  1647.8 4.5 add_convert_fusion
  1657.0 12.3 add_convert_fusion.5
  1669.3 7.3 reduce-scatter.36.cloned.1.call-done
  1681.9 31.9 %reduce-scatter.32.cloned.1.call-done = bf16[128,2]{1,0:T(8,128)(2,1)} async-done(((bf16[1024,2]{1,0:T(8,128)(2,1)}), bf16[128,2]{1,0:T(8,128)(2,1)}) %reduce-scatter.32.cloned.1.call-update) | async-done | bytes 528
  1714.6 35.7 %reduce-scatter.34.cloned.1.call-done = bf16[128,6]{1,0:T(8,128)(2,1)} async-done(((bf16[1024,6]{1,0:T(8,128)(2,1)}), bf16[128,6]{1,0:T(8,128)(2,1)}) %reduce-scatter.34.cloned.1.call-update) | async-done | bytes 1552
  1751.2 11.8 all-reduce.2
  1773.8 58.8 %all-gather.29.cloned.1.call-done = bf16[4096,512]{1,0:T(8,128)(2,1)} async-done(((bf16[1024,512]{1,0:T(8,128)(2,1)}), bf16[4096,512]{1,0:T(8,128)(2,1)}) %all-gather.29.cloned.1.call-update) | async-done | bytes 4194320 | tf_op jit(solution)/shard_map/all_gather | solution.py:285
  (372 shorter events, 314.3 us)
Async XLA Ops:
  7.2 99.5 %all-gather.15.cloned.1.call-start = ((), (), s32[]{:S(2)}) async-start(), calls=%async_computation.9 | async-start | bytes 5242880 | tf_op jit(solution)/shard_map/all_gather | solution.py:142
  8.7 10.2 copy-start.23
  10.3 8.5 copy-start.30
  11.1 7.7 copy-start.25
  12.7 6.1 copy-start.35
  12.8 287.5 %copy-start.33 = (f32[1,1024]{1,0:T(1,128)}, f32[1,1024]{1,0:T(1,128)S(1)}, u32[]{:S(2)}) copy-start(f32[1,1024]{1,0:T(1,128)S(1)} %get-tuple-element.416) | copy-start | bytes 12292
  21.5 4.8 copy-start.42
  23.1 165.0 %all-gather.17.cloned.1.call-start = ((), (), s32[]{:S(2)}) async-start(), calls=%async_computation.10 | async-start | bytes 5242880 | tf_op jit(solution)/shard_map/all_gather | solution.py:141
  25.9 608.6 %reduce-scatter.20.cloned.1.call-start = ((), (), s32[]{:S(2)}) async-start(), calls=%async_computation.11 | async-start | bytes 5242880 | tf_op jit(solution)/shard_map/reduce_scatter | solution.py:193
  194.6 102.7 %copy-start.3 = (bf16[512,1024]{1,0:T(8,128)(2,1)S(1)}, bf16[512,1024]{1,0:T(8,128)(2,1)}, u32[]{:S(2)}) copy-start(bf16[512,1024]{1,0:T(8,128)(2,1)} %param.21) | copy-start | bytes 3145732
  194.6 102.7 %copy-start.14 = (bf16[1024,1024]{1,0:T(8,128)(2,1)S(1)}, bf16[1024,1024]{1,0:T(8,128)(2,1)}, u32[]{:S(2)}) copy-start(bf16[1024,1024]{1,0:T(8,128)(2,1)} %param.24) | copy-start | bytes 6291460
  299.9 30.8 %copy-start.1 = (f32[512,1024]{1,0:T(8,128)}, f32[512,1024]{1,0:T(8,128)S(1)}, u32[]{:S(2)}) copy-start(f32[512,1024]{1,0:T(8,128)S(1)} %get-tuple-element.425) | copy-start | bytes 6291460
  300.2 10.8 copy-start.17
  300.2 10.8 copy-start.43
  300.3 24.8 %slice-start = ((s8[8388608]{0:T(1024)(128)(4,1)}), s8[4194304]{0:T(1024)(128)(4,1)S(1)}, s32[]{:S(2)}) async-start(s8[8388608]{0:T(1024)(128)(4,1)} %bitcast.236), calls=%async_computation.27 | async-start | bytes 8388608
  311.0 14.0 slice-start.1
  325.0 5.7 copy-start.48
  341.5 3.4 copy-start
  357.2 3.3 copy-start.10
  369.3 3.4 copy-start
  385.0 3.3 copy-start.10
  397.1 3.4 copy-start
  412.9 3.3 copy-start.10
  425.0 3.4 copy-start
  440.7 3.3 copy-start.10
  452.8 3.5 copy-start
  468.6 3.3 copy-start.10
  480.7 3.4 copy-start
  508.5 3.5 copy-start
  524.3 3.3 copy-start.10
  536.4 3.4 copy-start
  552.1 3.3 copy-start.10
  559.2 154.8 %reduce-scatter.22.cloned.1.call-start = ((), (), s32[]{:S(2)}) async-start(), calls=%async_computation.12 | async-start | bytes 5242880 | tf_op jit(solution)/shard_map/reduce_scatter | solution.py:196
  559.8 199.6 %reduce-scatter.30.cloned.1.call-start = ((), (), s32[]{:S(2)}) async-start(), calls=%async_computation.22 | async-start | bytes 2359296
  563.6 150.4 %copy-start.4 = (bf16[512,1024]{1,0:T(8,128)(2,1)S(1)}, bf16[512,1024]{1,0:T(8,128)(2,1)}, u32[]{:S(2)}) copy-start(bf16[512,1024]{1,0:T(8,128)(2,1)} %param.21) | copy-start | bytes 3145732
  563.6 150.4 %copy-start.19 = (bf16[8,512,2,64]{1,3,2,0:T(8,128)(2,1)S(1)}, bf16[8,512,2,64]{1,3,2,0:T(8,128)(2,1)}, u32[]{:S(2)}) copy-start(bf16[8,512,2,64]{1,3,2,0:T(8,128)(2,1)} %get-tuple-element.137) | copy-start | bytes 3145732
  563.6 150.4 %copy-start.24 = (f32[512]{0:T(512)S(1)}, f32[512]{0:T(512)}, u32[]{:S(2)}) copy-start(f32[512]{0:T(512)} %copy-done.23) | copy-start | bytes 6148
  563.6 150.4 %copy-start.26 = (f32[1,1024]{1,0:T(1,128)S(1)}, f32[1,1024]{1,0:T(1,128)}, u32[]{:S(2)}) copy-start(f32[1,1024]{1,0:T(1,128)} %copy-done.25) | copy-start | bytes 12292
  563.6 150.4 %copy-start.31 = (f32[512]{0:T(512)S(1)}, f32[512]{0:T(512)}, u32[]{:S(2)}) copy-start(f32[512]{0:T(512)} %copy-done.30) | copy-start | bytes 6148
  563.6 150.4 %copy-start.36 = (f32[1,1024]{1,0:T(1,128)S(1)}, f32[1,1024]{1,0:T(1,128)}, u32[]{:S(2)}) copy-start(f32[1,1024]{1,0:T(1,128)} %copy-done.35) | copy-start | bytes 12292
  567.9 256.4 %reduce-scatter.28.cloned.1.call-start = ((), (), s32[]{:S(2)}) async-start(), calls=%async_computation.21 | async-start | bytes 7077888
  730.8 168.4 %reduce-scatter.26.cloned.1.call-start = ((), (), s32[]{:S(2)}) async-start(), calls=%async_computation.14 | async-start | bytes 9437184 | tf_op jit(solution)/shard_map/reduce_scatter | solution.py:231
  743.4 230.6 %reduce-scatter.24.cloned.1.call-start = ((), (), s32[]{:S(2)}) async-start(), calls=%async_computation.13 | async-start | bytes 9437184 | tf_op jit(solution)/shard_map/reduce_scatter | solution.py:228
  754.2 344.6 %all-reduce.6.cloned.1.call-start = ((), (), s32[]{:S(2)}) async-start(), calls=%async_computation.26 | async-start | bytes 6291456 | tf_op jit(solution)/shard_map/psum | solution.py:245
  974.0 229.1 %all-gather.19.cloned.1.call-start = ((), (), s32[]{:S(2)}) async-start(), calls=%async_computation.15 | async-start | bytes 18874368 | tf_op jit(solution)/shard_map/all_gather | solution.py:272
  1101.2 3.3 copy-start.6
  1101.2 3.3 copy-start.12
  1114.2 199.8 %all-gather.21.cloned.1.call-start = ((), (), s32[]{:S(2)}) async-start(), calls=%async_computation.16 | async-start | bytes 18874368 | tf_op jit(solution)/shard_map/all_gather | solution.py:272
  1224.1 197.6 %all-gather.23.cloned.1.call-start = ((), (), s32[]{:S(2)}) async-start(), calls=%async_computation.17 | async-start | bytes 18874368 | tf_op jit(solution)/shard_map/all_gather | solution.py:272
  1331.8 197.6 %all-gather.25.cloned.1.call-start = ((), (), s32[]{:S(2)}) async-start(), calls=%async_computation.18 | async-start | bytes 18874368 | tf_op jit(solution)/shard_map/all_gather | solution.py:272
  1439.5 197.6 %all-gather.27.cloned.1.call-start = ((), (), s32[]{:S(2)}) async-start(), calls=%async_computation.19 | async-start | bytes 18874368 | tf_op jit(solution)/shard_map/all_gather | solution.py:272
  1547.2 129.5 %reduce-scatter.36.cloned.1.call-start = ((), (), s32[]{:S(2)}) async-start(), calls=%async_computation.25 | async-start | bytes 1179648
  1548.8 11.6 copy-start.38
  1548.9 11.6 copy-start.29
  1548.9 11.6 copy-start.28
  1548.9 164.9 %reduce-scatter.32.cloned.1.call-start = ((), (), s32[]{:S(2)}) async-start(), calls=%async_computation.23 | async-start | bytes 294912
  1558.9 191.4 %reduce-scatter.34.cloned.1.call-start = ((), (), s32[]{:S(2)}) async-start(), calls=%async_computation.24 | async-start | bytes 294912
  1563.0 269.5 %all-gather.29.cloned.1.call-start = ((), (), s32[]{:S(2)}) async-start(), calls=%async_computation.20 | async-start | bytes 5242880 | tf_op jit(solution)/shard_map/all_gather | solution.py:285
  1652.3 4.6 copy-start.32
  1669.3 93.7 %copy-start.41 = (f32[2,128]{1,0:T(2,128)S(1)}, f32[2,128]{1,0:T(2,128)}, u32[]{:S(2)}) copy-start(f32[2,128]{1,0:T(2,128)} %param.35) | copy-start | bytes 3076
  1669.3 94.9 %copy-start.40 = (f32[512]{0:T(512)S(1)}, f32[512]{0:T(512)}, u32[]{:S(2)}) copy-start(f32[512]{0:T(512)} %param.37) | copy-start | bytes 6148
  1669.3 95.6 %copy-start.37 = (f32[6,128]{1,0:T(8,128)S(1)}, f32[6,128]{1,0:T(8,128)}, u32[]{:S(2)}) copy-start(f32[6,128]{1,0:T(8,128)} %param.36) | copy-start | bytes 9220
  1681.9 90.1 %copy-start.5 = (f32[512,1024]{0,1:T(8,128)S(1)}, f32[512,1024]{0,1:T(8,128)}, u32[]{:S(2)}) copy-start(f32[512,1024]{0,1:T(8,128)} %get-tuple-element.414) | copy-start | bytes 6291460
  1769.0 63.5 %copy-start.13 = (bf16[512,1024]{0,1:T(8,128)(2,1)S(1)}, bf16[512,1024]{0,1:T(8,128)(2,1)}, u32[]{:S(2)}) copy-start(bf16[512,1024]{0,1:T(8,128)(2,1)} %copy.91) | copy-start | bytes 3145732
  (26 other events, 48.4 us)
Sparse Core Ops, SparseCore 0:
  23.3 83.4 all-gather.14
  108.9 79.2 all-gather.16
  559.3 75.1 reduce-scatter.19
  636.7 77.2 reduce-scatter.21
  717.7 41.6 reduce-scatter.29
  762.6 61.6 reduce-scatter.27
  827.8 71.3 reduce-scatter.25
  902.6 71.2 reduce-scatter.23
  977.7 121.0 all-reduce.5
  1114.3 88.7 all-gather.18
  1224.2 89.7 all-gather.20
  1331.9 89.7 all-gather.22
  1439.6 89.7 all-gather.24
  1547.3 89.7 all-gather.26
  1640.6 35.9 reduce-scatter.35
  1680.1 33.6 reduce-scatter.31
  1716.6 33.6 reduce-scatter.33
  1751.8 80.7 all-gather.28
